TPU v7x, 32 devices: a 4x2x2 block of a 4x4x8 slice. The times are simulated.
32 devices in a mesh: dp: 4 (over y, z), tp: 8 (over x, core).
Axes of the slice: x: 4, y: 2, z: 2, core: 2. Of those that a mesh axis runs over, the one named last changes fastest.
The devices are a block of a 4x4x8 slice.
Arguments:
- token_ids: int32 [32768], P('dp'), parts along dimension 0
- positions: int32 [32768], P('dp'), parts along dimension 0
- embed_table: bfloat16 [257216, 2048], P('tp')
- norm_scale: float32 [2048], replicated
- w_query: bfloat16 [2048, 2048], P(None, 'tp')
- w_key: bfloat16 [2048, 256], replicated
- w_value: bfloat16 [2048, 256], replicated
Outputs:
- output 1: bfloat16 [32768, 2048], P(('dp', 'tp')), parts along dimension 0
- output 2: bfloat16 [32768, 8, 256], P('dp', 'tp'), parts along dimension 0
- output 3: bfloat16 [32768, 8, 256], P('dp', 'tp'), parts along dimension 0
- output 4: bfloat16 [32768, 8, 256], P('dp', 'tp'), parts along dimension 0
There are 4 independent parts. A program takes and returns all parts, laid end to end along the dimension named above; an argument that names none is the same for every part.
All inputs are finite; a program needn't handle non-finite values.
Results may differ from a plain program's by a relative error of at most 0.0120276.
Values are sent between devices in bfloat16 or wider.
A program may use at most 768 MiB of HBM per device.

v0:
```python
import math
import jax
import jax.numpy as jnp
from jax import lax
from jax.sharding import PartitionSpec as P

HEAD_DIM = 256
EPSILON = 1e-6
ROPE_BASE = 10000.0


def rope_tables(positions):
    inv_freq = ROPE_BASE ** (-jnp.arange(0, HEAD_DIM, 2, dtype=jnp.float32) / HEAD_DIM)
    angles = positions.astype(jnp.float32)[:, None] * inv_freq[None, :]
    return jnp.cos(angles)[:, None, :], jnp.sin(angles)[:, None, :]


def rotate(head_vals, cosines, sines):
    half_dim = head_vals.shape[-1] // 2
    front_half = head_vals[..., :half_dim]
    back_half = head_vals[..., half_dim:]
    return jnp.concatenate([front_half * cosines - back_half * sines, back_half * cosines + front_half * sines], axis=-1)


def rms_norm(resid_rows, norm_scale):
    widened = resid_rows.astype(jnp.float32)
    inv_rms = lax.rsqrt(jnp.mean(widened * widened, axis=-1, keepdims=True) + EPSILON)
    return (widened * inv_rms * (1.0 + norm_scale)).astype(jnp.bfloat16)


def project(normed, weight, cosines, sines, factor):
    linear = jnp.dot(normed, weight, preferred_element_type=jnp.float32).astype(jnp.bfloat16)
    head_view = linear.reshape(linear.shape[0], -1, HEAD_DIM).astype(jnp.float32)
    return (rotate(head_view, cosines, sines) * factor).astype(jnp.bfloat16)


def solution(mesh):
    group_size = mesh.shape["tp"]

    def local_step(token_ids, positions, table_rows, norm_scale, w_query, w_key, w_value):
        dev_index = lax.axis_index("tp")
        vocab_rows, model_width = table_rows.shape
        normalizer = jnp.asarray(math.sqrt(model_width), dtype=jnp.bfloat16)
        local_ids = token_ids - dev_index * vocab_rows
        inside = (local_ids >= 0) & (local_ids < vocab_rows)
        picked = jnp.take(table_rows, local_ids, axis=0, mode="clip") * normalizer
        partial = jnp.where(inside[:, None], picked, jnp.zeros((), jnp.bfloat16))
        residual = lax.psum_scatter(partial, "tp", scatter_dimension=0, tiled=True)
        normed = lax.all_gather(rms_norm(residual, norm_scale), "tp", axis=0, tiled=True)
        cosines, sines = rope_tables(positions)
        queries = project(normed, w_query, cosines, sines, HEAD_DIM ** -0.5)
        kv_heads = w_key.shape[1] // HEAD_DIM
        slot_count = max(kv_heads, group_size)
        slots_here = slot_count // group_size
        first_head = (dev_index * slots_here) // (slot_count // kv_heads)
        key_cols = lax.dynamic_slice_in_dim(w_key, first_head * HEAD_DIM, slots_here * HEAD_DIM, axis=1)
        value_cols = lax.dynamic_slice_in_dim(w_value, first_head * HEAD_DIM, slots_here * HEAD_DIM, axis=1)
        key_heads = project(normed, key_cols, cosines, sines, 1.0)
        value_lin = jnp.dot(normed, value_cols, preferred_element_type=jnp.float32).astype(jnp.bfloat16)
        value_heads = value_lin.reshape(value_lin.shape[0], slots_here, HEAD_DIM)
        return residual, queries, key_heads, value_heads

    head_spec = P("dp", "tp", None)
    return jax.shard_map(local_step, mesh=mesh, in_specs=(P("dp"), P("dp"), P("tp", None), P(), P(None, "tp"), P(), P()), out_specs=(P(("dp", "tp"), None), head_spec, head_spec, head_spec), check_vma=False)
```

profile of v0, /device:TPU:125, one launch (start us, length us, event | category | flops | bytes accessed | tf_op | source)
XLA Modules:
  0.0 899.0 jit_solution(16075122224027816320)
XLA Ops:
  7.2 0.0 copy-start
  7.2 0.1 reduce-scatter.2.cloned.1.call-start
  7.3 0.8 compare_and_fusion
  8.1 0.8 subtract_clamp_fusion
  8.9 438.8 %gather_fusion = bf16[8192,2048]{1,0:T(8,128)(2,1)} fusion(bf16[32152,2048]{1,0:T(8,128)(2,1)} %param.9, s32[8192]{0:T(1024)S(1)} %subtract_clamp_fusion), kind=kCustom, calls=%fused_computation | custom fusion | bytes 67141632 | tf_op jit(solution)/shard_map/jit(_take)/gather | solution.py:46
  447.7 22.9 %multiply_select_fusion = bf16[8192,2048]{1,0:T(8,128)(2,1)} fusion(bf16[8192,2048]{1,0:T(8,128)(2,1)} %gather_fusion, pred[8192]{0:T(1024)(128)(4,1)S(1)} %compare_and_fusion), kind=kLoop, calls=%fused_computation.1 | loop fusion | flops 33554432 | bytes 67117056 | tf_op jit(solution)/shard_map/jit(_where)/select_n | solution.py:47
  470.5 0.0 copy-start.3
  470.5 0.1 reduce-scatter.2.cloned.1.call-update
  470.6 0.1 all-gather.2.cloned.1.call-start
  470.7 0.6 copy-done.3
  471.2 167.6 %reduce-scatter.2.cloned.1.call-done = bf16[1024,2048]{1,0:T(8,128)(2,1)} async-done(((bf16[8192,2048]{1,0:T(8,128)(2,1)}), bf16[1024,2048]{1,0:T(8,128)(2,1)}) %reduce-scatter.2.cloned.1.call-update) | async-done | bytes 4194320 | tf_op jit(solution)/shard_map/reduce_scatter | solution.py:48
  638.9 0.0 copy-start.1
  638.9 3.2 fusion.5
  642.1 0.2 copy-done.1
  642.3 3.0 fusion.7
  645.4 0.0 copy-start.2
  645.4 0.1 all-gather.2.cloned.1.call-update
  645.4 0.7 copy-done.2
  646.2 0.0 copy-start.4
  646.2 153.9 %all-gather.2.cloned.1.call-done = bf16[8192,2048]{1,0:T(8,128)(2,1)} async-done(((bf16[1024,2048]{1,0:T(8,128)(2,1)}), bf16[8192,2048]{1,0:T(8,128)(2,1)}) %all-gather.2.cloned.1.call-update) | async-done | bytes 33554448 | tf_op jit(solution)/shard_map/all_gather | solution.py:49
  800.1 0.0 copy-done
  800.1 17.5 %fusion.3 = f32[8192,1,256]{0,2,1:T(8,128)} fusion(bf16[8192,2048]{1,0:T(8,128)(2,1)} %all-gather.2.cloned.1.call-done, bf16[2048,256]{1,0:T(8,128)(2,1)S(1)} %copy-done), kind=kOutput, calls=%fused_computation.10 | convolution fusion | flops 8594128896 | bytes 42991616 | tf_op jit(solution)/shard_map/dot_general | solution.py:32
  817.6 0.0 copy-done.4
  817.6 17.5 %fusion.1 = f32[8192,1,256]{0,2,1:T(8,128)} fusion(bf16[8192,2048]{1,0:T(8,128)(2,1)} %all-gather.2.cloned.1.call-done, bf16[2048,256]{1,0:T(8,128)(2,1)S(1)} %copy-done.4), kind=kOutput, calls=%fused_computation.8 | convolution fusion | flops 8594128896 | bytes 42991616 | tf_op jit(solution)/shard_map/dot_general | solution.py:32
  835.1 20.2 %fusion.20 = (bf16[8192,1,128]{0,2,1:T(8,128)(2,1)S(1)}, bf16[8192,1,128]{0,2,1:T(8,128)(2,1)S(1)}, f32[8192,1,128]{0,2,1:T(8,128)}, f32[8192,1,128]{0,2,1:T(8,128)}) fusion(f32[8192,1,256]{0,2,1:T(8,128)} %fusion.3, f32[128]{0:T(128)S(1)} %multiply_power_fusion, f32[8192]{0:T(1024)S(1)} %convert_element_type.55, f32[8192,1,256]{0,2,1:T(8,128)} %fusion.1), kind=kLoop, calls=%fused_computation.30 | loop fusion | flops 15728640 | bytes 29393408 | tf_op jit(solution)/shard_map/convert.2
  855.2 2.5 pad_maximum_fusion
  857.7 6.4 copy.12
  864.1 5.1 fusion.8
  869.2 0.0 copy-start.5
  869.2 6.4 copy.11
  875.7 0.0 copy-done.5
  875.7 16.4 %fusion.4 = bf16[8192,1,256]{2,0,1:T(8,128)(2,1)} fusion(bf16[8192,2048]{1,0:T(8,128)(2,1)} %all-gather.2.cloned.1.call-done, bf16[2048,256]{1,0:T(8,128)(2,1)S(1)} %copy-done.5), kind=kOutput, calls=%fused_computation.11 | convolution fusion | flops 8592031744 | bytes 38797312 | tf_op jit(solution)/shard_map/dot_general | solution.py:59
  (4 shorter events, 0.0 us)
Async XLA Ops:
  7.2 792.9 %copy-start = (bf16[2048,256]{1,0:T(8,128)(2,1)S(1)}, bf16[2048,256]{1,0:T(8,128)(2,1)}, u32[]{:S(2)}) copy-start(bf16[2048,256]{1,0:T(8,128)(2,1)} %param.12) | copy-start | bytes 3145732
  7.2 631.7 %reduce-scatter.2.cloned.1.call-start = ((), (), s32[]{:S(2)}) async-start(), calls=%async_computation.1 | async-start | bytes 37748736 | tf_op jit(solution)/shard_map/reduce_scatter | solution.py:48
  470.5 0.7 copy-start.3
  470.6 329.5 %all-gather.2.cloned.1.call-start = ((), (), s32[]{:S(2)}) async-start(), calls=%async_computation.2 | async-start | bytes 37748736 | tf_op jit(solution)/shard_map/all_gather | solution.py:49
  638.9 3.4 copy-start.1
  645.4 0.8 copy-start.2
  646.2 171.4 %copy-start.4 = (bf16[2048,256]{1,0:T(8,128)(2,1)S(1)}, bf16[2048,256]{1,0:T(8,128)(2,1)}, u32[]{:S(2)}) copy-start(bf16[2048,256]{1,0:T(8,128)(2,1)} %param.11) | copy-start | bytes 3145732
  869.2 6.5 copy-start.5
Sparse Core Ops, SparseCore 0:
  470.7 168.1 reduce-scatter.1
  645.6 154.4 all-gather.1
where the time goes:
time: 910 us; the launch traced here: 899 us
  local copies, waits for them, and re-layouts  453 us (50%)
  waiting for transfers between devices  322 us (35%)
  other arithmetic  58.5 us (6%)
  matrix products  51.4 us (6%)
  between operations  14.1 us (2%)
    gather x1, local copies, waits for them, and re-layouts, local_step(): picked = jnp.take(table_rows, local_ids, axis=0, mode='clip') * normalizer  439 us
    reduce_scatter x1, waiting for transfers between devices, local_step(): residual = lax.psum_scatter(partial, 'tp', scatter_dimension=0, tiled=True)  168 us
    all_gather x1, waiting for transfers between devices, local_step(): lax.all_gather(rms_norm(residual, norm_scale), 'tp', axis=0, tiled=True)  154 us
    dot_general x2, matrix products, project(): jnp.dot(normed, weight, preferred_element_type=jnp.float32)  35 us
    select_n x1, other arithmetic, local_step(): partial = jnp.where(inside[:, None], picked, jnp.zeros((), jnp.bfloat16))  22.9 us
    another operation x1, other arithmetic  20.2 us
  transfers between devices with their start and end apart: 2, of which 2 were waited for; matrix products, arithmetic and copies ran while one was open for 0% of the time, Pallas kernels for 0%

commit v1 on v0

v1 whole, which is shorter than its diff:
```python
import functools
import math
import jax
import jax.numpy as jnp
import numpy as np
from jax import lax
from jax.experimental import pallas as pl
from jax.experimental.pallas import tpu as pltpu
from jax.sharding import PartitionSpec as P

HEAD_DIM = 256
EPSILON = 1e-6
ROPE_BASE = 10000.0
CHUNK = 64
PICK = 32
SLAB = 8
DEPTH = 4
CORES = 2
VMEM_LIMIT = 60 * 1024 * 1024


def rope_tables(positions):
    inv_freq = ROPE_BASE ** (-jnp.arange(0, HEAD_DIM, 2, dtype=jnp.float32) / HEAD_DIM)
    angles = positions.astype(jnp.float32)[:, None] * inv_freq[None, :]
    return jnp.cos(angles), jnp.sin(angles)


def rms_norm(resid_rows, norm_scale):
    widened = resid_rows.astype(jnp.float32)
    inv_rms = lax.rsqrt(jnp.mean(widened * widened, axis=-1, keepdims=True) + EPSILON)
    return (widened * inv_rms * (1.0 + norm_scale)).astype(jnp.bfloat16)


def rotate(head_vals, cosines, sines):
    half_dim = head_vals.shape[-1] // 2
    front_half = head_vals[..., :half_dim]
    back_half = head_vals[..., half_dim:]
    return jnp.concatenate([front_half * cosines - back_half * sines, back_half * cosines + front_half * sines], axis=-1)


def project(normed, weight, cosines, sines, factor):
    linear = jnp.dot(normed, weight, preferred_element_type=jnp.float32).astype(jnp.bfloat16)
    head_view = linear.reshape(linear.shape[0], -1, HEAD_DIM).astype(jnp.float32)
    return (rotate(head_view, cosines, sines) * factor).astype(jnp.bfloat16)


def dense_path(token_ids, positions, table_rows, norm_scale, w_query, key_cols, value_cols):
    dev_index = lax.axis_index("tp")
    vocab_rows, model_width = table_rows.shape
    normalizer = jnp.asarray(math.sqrt(model_width), dtype=jnp.bfloat16)
    local_ids = token_ids - dev_index * vocab_rows
    inside = (local_ids >= 0) & (local_ids < vocab_rows)
    picked = jnp.take(table_rows, local_ids, axis=0, mode="clip") * normalizer
    partial = jnp.where(inside[:, None], picked, jnp.zeros((), jnp.bfloat16))
    residual = lax.psum_scatter(partial, "tp", scatter_dimension=0, tiled=True)
    normed = lax.all_gather(rms_norm(residual, norm_scale), "tp", axis=0, tiled=True)
    cosines, sines = rope_tables(positions)
    cosines, sines = cosines[:, None, :], sines[:, None, :]
    queries = project(normed, w_query, cosines, sines, HEAD_DIM ** -0.5)
    key_heads = project(normed, key_cols, cosines, sines, 1.0)
    value_lin = jnp.dot(normed, value_cols, preferred_element_type=jnp.float32).astype(jnp.bfloat16)
    return residual, queries[:, 0, :], key_heads[:, 0, :], value_lin


class Plan:
    def __init__(self, group_size, tokens, vocab_rows):
        unit = CHUNK * 2
        self.hot = min(tokens // 8, vocab_rows // unit * unit)
        share = [11 / 32, 5 / 64] + [3 / 64] * 2
        room = [share[o] if o < 4 else 3 / 128 for o in range(group_size)]
        self.caps = [max(CHUNK, -(-int(tokens * r) // CHUNK) * CHUNK) for r in room]
        self.bases, at = [], self.hot
        for cap in self.caps:
            self.bases.append(at)
            at += cap
        self.rows = at
        self.list_rows = -(-(-(-max(self.caps) // 128)) // 8) * 8


def choose(values, index):
    out = jnp.int32(values[0])
    for j in range(1, len(values)):
        out = jnp.where(index == j, jnp.int32(values[j]), out)
    return out


def prep_kernel(plan, group_size, vocab_rows, ids_ref, slot_ref, list_ref, count_ref):
    me = lax.axis_index("tp")
    ids = ids_ref[...]
    blocks, lanes = ids.shape
    cold = ids >= plan.hot
    masks = [cold & (ids >= o * vocab_rows) & (ids < (o + 1) * vocab_rows) for o in range(group_size)]
    stack = jnp.concatenate([m.astype(jnp.float32) for m in masks], axis=0)
    stack = stack.astype(jnp.bfloat16)
    tri_r = lax.broadcasted_iota(jnp.int32, (lanes, lanes), 0)
    tri_c = lax.broadcasted_iota(jnp.int32, (lanes, lanes), 1)
    upper = (tri_r <= tri_c).astype(jnp.float32).astype(jnp.bfloat16)
    within = jnp.dot(stack, upper, preferred_element_type=jnp.float32)
    totals = jnp.dot(stack, jnp.ones((lanes, lanes), jnp.bfloat16), preferred_element_type=jnp.float32)
    low_r = lax.broadcasted_iota(jnp.int32, (blocks, blocks), 0)
    low_c = lax.broadcasted_iota(jnp.int32, (blocks, blocks), 1)
    lower = (low_c < low_r).astype(jnp.float32).astype(jnp.bfloat16)
    slot = jnp.where(cold, 0, ids)
    own_rank = jnp.full((blocks, lanes), -1, jnp.int32)
    for o in range(group_size):
        tot = totals[o * blocks:(o + 1) * blocks]
        before = jnp.dot(lower, tot.astype(jnp.bfloat16), preferred_element_type=jnp.float32)
        rank = (before + within[o * blocks:(o + 1) * blocks]).astype(jnp.int32) - 1
        slot = slot + jnp.where(masks[o], jnp.minimum(rank, plan.caps[o] - 1) + plan.bases[o], 0)
        own_rank = jnp.where(masks[o] & (me == o), rank, own_rank)
        count_ref[o:o + 1, :] = (before[blocks - 1:] + tot[blocks - 1:]).astype(jnp.int32)
    slot_ref[...] = slot
    local = jnp.where(own_rank >= 0, ids - me * vocab_rows, 0)
    major, minor = own_rank >> 7, own_rank & 127
    high, low = local >> 8, local & 255
    iota_major = lax.broadcasted_iota(jnp.int32, (plan.list_rows, lanes), 0)
    iota_minor = lax.broadcasted_iota(jnp.int32, (lanes, lanes), 0)
    acc = jnp.zeros((2 * plan.list_rows, lanes), jnp.float32)
    per = 8
    for g in range(blocks // per):
        lhs, rhs = [], []
        for r in range(g * per, (g + 1) * per):
            hit = iota_major == major[r:r + 1, :]
            lhs.append(jnp.concatenate([jnp.where(hit, high[r:r + 1, :], 0), jnp.where(hit, low[r:r + 1, :], 0)], axis=0).astype(jnp.float32))
            rhs.append((iota_minor == minor[r:r + 1, :]).astype(jnp.float32))
        left = jnp.concatenate(lhs, axis=1).astype(jnp.bfloat16)
        right = jnp.concatenate(rhs, axis=1).astype(jnp.bfloat16)
        acc = acc + lax.dot_general(left, right, (((1,), (1,)), ((), ())), preferred_element_type=jnp.float32)
    whole = acc.astype(jnp.int32)
    list_ref[...] = whole[:plan.list_rows] * 256 + whole[plan.list_rows:]


def prepare(plan, group_size, vocab_rows, token_ids):
    blocks = token_ids.shape[0] // 128
    return pl.pallas_call(
        functools.partial(prep_kernel, plan, group_size, vocab_rows),
        out_shape=(
            jax.ShapeDtypeStruct((blocks, 128), jnp.int32),
            jax.ShapeDtypeStruct((plan.list_rows, 128), jnp.int32),
            jax.ShapeDtypeStruct((group_size, 128), jnp.int32),
        ),
        compiler_params=pltpu.CompilerParams(vmem_limit_bytes=VMEM_LIMIT),
        name="slots",
    )(token_ids.reshape(blocks, 128))


def pick_rows(rows_smem, total, source, emit, slabs, onehot, sem):
    groups = (total + PICK - 1) // PICK

    def fetch(g):
        place = lax.rem(g, DEPTH)
        lane = lax.broadcasted_iota(jnp.int32, (1, PICK * SLAB), 1)
        for i in range(PICK):
            row = rows_smem[g * PICK + i]
            start = pl.multiple_of((row >> 3) << 3, SLAB)
            pltpu.make_async_copy(source.at[pl.ds(start, SLAB)], slabs.at[place, pl.ds(i * SLAB, SLAB)], sem.at[place]).start()
            onehot[place, pl.ds(i, 1), :] = jnp.where(lane == (row & 7) + i * SLAB, 1.0, 0.0)

    for g in range(DEPTH - 1):
        @pl.when(g < groups)
        def _():
            fetch(g)

    def body(g, carry):
        place = lax.rem(g, DEPTH)

        @pl.when(g + DEPTH - 1 < groups)
        def _():
            fetch(g + DEPTH - 1)

        pltpu.make_async_copy(source.at[pl.ds(0, PICK * SLAB)], slabs.at[place], sem.at[place]).wait()
        picked = jnp.dot(onehot[place].astype(jnp.bfloat16), slabs[place], preferred_element_type=jnp.float32)
        emit(g, picked)
        return carry

    lax.fori_loop(0, groups, body, 0)
    return groups


def gather_kernel(plan, normalizer, counts, rows_smem, table, out, slabs, onehot, stage, hot_in, sem, out_sem, hot_sem):
    me = lax.axis_index("tp")
    total = jnp.minimum(counts[me], choose(plan.caps, me))
    base = choose(plan.bases, me)
    scale = jnp.float32(normalizer)

    def emit(g, picked):
        side = lax.rem(g, 2)

        @pl.when(g >= 2)
        def _():
            pltpu.make_async_copy(stage.at[side], out.at[pl.ds(0, PICK)], out_sem.at[side]).wait()

        stage[side] = (picked * scale).astype(jnp.bfloat16)
        at = pl.multiple_of(base + g * PICK, PICK)
        pltpu.make_async_copy(stage.at[side], out.at[pl.ds(at, PICK)], out_sem.at[side]).start()

    @pl.when(me == 0)
    def _():
        step = hot_in.shape[1]
        n_steps = plan.hot // step
        def load(i):
            return pltpu.make_async_copy(table.at[pl.ds(i * step, step)], hot_in.at[i % 2], hot_sem.at[i % 2])
        def save(i):
            return pltpu.make_async_copy(hot_in.at[i % 2], out.at[pl.ds(i * step, step)], hot_sem.at[2 + i % 2])
        load(0).start()
        for i in range(n_steps):
            if i + 1 < n_steps:
                if i >= 1:
                    save(i - 1).wait()
                load(i + 1).start()
            load(i).wait()
            hot_in[i % 2] = (hot_in[i % 2].astype(jnp.float32) * scale).astype(jnp.bfloat16)
            save(i).start()
        if n_steps > 1:
            save(n_steps - 2).wait()
        save(n_steps - 1).wait()

    groups = pick_rows(rows_smem, total, table, emit, slabs, onehot, sem)
    for last in (2, 1):
        @pl.when(groups >= last)
        def _():
            side = lax.rem(groups - last, 2)
            pltpu.make_async_copy(stage.at[side], out.at[pl.ds(0, PICK)], out_sem.at[side]).wait()


def gather_rows(plan, normalizer, counts, rows, table):
    width = table.shape[1]
    hot_step = min(256, plan.hot)
    return pl.pallas_call(
        functools.partial(gather_kernel, plan, normalizer),
        out_shape=jax.ShapeDtypeStruct((plan.rows, width), table.dtype),
        in_specs=[pl.BlockSpec(memory_space=pltpu.SMEM), pl.BlockSpec(memory_space=pltpu.SMEM), pl.BlockSpec(memory_space=pl.ANY)],
        out_specs=pl.BlockSpec(memory_space=pl.ANY),
        scratch_shapes=[
            pltpu.VMEM((DEPTH, PICK * SLAB, width), table.dtype),
            pltpu.VMEM((DEPTH, PICK, PICK * SLAB), jnp.float32),
            pltpu.VMEM((2, PICK, width), table.dtype),
            pltpu.VMEM((2, hot_step, width), table.dtype),
            pltpu.SemaphoreType.DMA((DEPTH,)),
            pltpu.SemaphoreType.DMA((2,)),
            pltpu.SemaphoreType.DMA((4,)),
        ],
        compiler_params=pltpu.CompilerParams(vmem_limit_bytes=VMEM_LIMIT),
        cost_estimate=pl.CostEstimate(flops=2 * 2048 * 256 * 2816, bytes_accessed=100_000_000, transcendentals=0),
        name="owner_rows",
    )(counts, rows, table)


def resid_kernel(rows_smem, source, out, slabs, onehot, sem, *, count):
    def emit(g, picked):
        at = pl.multiple_of(g * PICK, PICK)
        out[pl.ds(at, PICK), :] = picked.astype(out.dtype)
    pick_rows(rows_smem, count, source, emit, slabs, onehot, sem)


def own_rows(source, rows):
    width, count = source.shape[1], rows.shape[0]
    return pl.pallas_call(
        functools.partial(resid_kernel, count=count),
        out_shape=jax.ShapeDtypeStruct((count, width), source.dtype),
        in_specs=[pl.BlockSpec(memory_space=pltpu.SMEM), pl.BlockSpec(memory_space=pl.ANY)],
        out_specs=pl.BlockSpec(memory_space=pltpu.VMEM),
        scratch_shapes=[
            pltpu.VMEM((DEPTH, PICK * SLAB, width), source.dtype),
            pltpu.VMEM((DEPTH, PICK, PICK * SLAB), jnp.float32),
            pltpu.SemaphoreType.DMA((DEPTH,)),
        ],
        compiler_params=pltpu.CompilerParams(vmem_limit_bytes=VMEM_LIMIT),
        name="own_residual",
    )(rows, source)


def multicast_kernel(plan, group_size, buf_in, buf, got, ring_sem, pair_sem):
    del buf_in
    chips = group_size // CORES
    me = lax.axis_index("tp")
    chip, core = lax.div(me, CORES), lax.rem(me, CORES)
    mate = chip * CORES + (1 - core)
    step = 1 - 2 * core

    def chip_at(delta):
        return lax.rem(chip + delta * step + 2 * chips, chips)

    ahead, behind = chip_at(1) * CORES + core, chip_at(-1) * CORES + core

    barrier = pltpu.get_barrier_semaphore()
    for other in (mate, ahead, behind):
        pl.semaphore_signal(barrier, inc=1, device_id={"tp": other}, device_id_type=pl.DeviceIdType.MESH)
    pl.semaphore_wait(barrier, 3)

    own_n = [c // CHUNK for c in plan.caps]
    own_n[0] += plan.hot // CHUNK
    own_at, at = [], 0
    for c in own_n:
        own_at.append(at)
        at += c
    first = [own_at[2 * c] for c in range(chips)]
    half = [(own_n[2 * c] + own_n[2 * c + 1]) // 2 for c in range(chips)]
    turn = [own_n[2 * c] - half[c] for c in range(chips)]

    def rows(j):
        return pl.ds(pl.multiple_of(j * CHUNK, CHUNK), CHUNK)

    def ring(j):
        return pltpu.make_async_remote_copy(src_ref=buf.at[rows(j)], dst_ref=buf.at[rows(j)], send_sem=ring_sem.at[j], recv_sem=got.at[j], device_id={"tp": ahead}, device_id_type=pl.DeviceIdType.MESH)

    def pair(j):
        return pltpu.make_async_remote_copy(src_ref=buf.at[rows(j)], dst_ref=buf.at[rows(j)], send_sem=pair_sem.at[j], recv_sem=got.at[j], device_id={"tp": mate}, device_id_type=pl.DeviceIdType.MESH)

    def loop(count, fn):
        def body(t, c):
            fn(t)
            return c
        lax.fori_loop(0, count, body, 0)

    my_first, my_half, my_turn = choose(first, chip), choose(half, chip), choose(turn, chip)
    mine = jnp.where(core == 0, my_half, my_half - my_turn)
    mine_at = jnp.where(core == 0, my_first, my_first + my_half + my_turn)
    cross_at = my_first + my_half

    @pl.when(core == 0)
    def _():
        loop(my_turn, lambda t: pair(cross_at + t).start())

    loop(mine, lambda t: ring(mine_at + t).start())
    loop(mine, lambda t: pair(mine_at + t).start())

    @pl.when(core == 1)
    def _():
        def relay(t):
            pair(cross_at + t).wait_recv()
            ring(cross_at + t).start()
        loop(my_turn, relay)

    for hop in range(1, chips):
        origin = chip_at(-hop)
        count = choose(half, origin)
        base = choose(first, origin) + core * count
        shift = core * choose(turn, origin)

        def arrive(t):
            j = base + lax.rem(t + shift, count)
            ring(j).wait_recv()
            if hop < chips - 1:
                ring(j).start()
            pair(j).start()
        loop(count, arrive)

    for hop in range(1, chips):
        origin = lax.rem(chip - hop * step + 2 * chips, chips)
        count = choose(half, origin)
        base = choose(first, origin) + (1 - core) * count
        loop(count, lambda t: pair(base + t).wait_recv())
    theirs = jnp.where(core == 0, my_half - my_turn, my_half)
    theirs_at = jnp.where(core == 0, my_first + my_half + my_turn, my_first)
    loop(theirs, lambda t: pair(theirs_at + t).wait_recv())

    @pl.when(core == 0)
    def _():
        loop(my_turn, lambda t: pair(cross_at + t).wait_send())

    @pl.when(core == 1)
    def _():
        loop(my_turn, lambda t: ring(cross_at + t).wait_send())

    def sent(t):
        ring(mine_at + t).wait_send()
        pair(mine_at + t).wait_send()
    loop(mine, sent)
    for hop in range(1, chips):
        origin = chip_at(-hop)
        count = choose(half, origin)
        base = choose(first, origin) + core * count

        def left(t):
            if hop < chips - 1:
                ring(base + t).wait_send()
            pair(base + t).wait_send()
        loop(count, left)


def multicast(plan, group_size, buf):
    chunks = plan.rows // CHUNK
    return pl.pallas_call(
        functools.partial(multicast_kernel, plan, group_size),
        out_shape=jax.ShapeDtypeStruct(buf.shape, buf.dtype),
        in_specs=[pl.BlockSpec(memory_space=pl.ANY)],
        out_specs=pl.BlockSpec(memory_space=pl.ANY),
        scratch_shapes=[pltpu.SemaphoreType.DMA((chunks,)), pltpu.SemaphoreType.DMA((chunks,)), pltpu.SemaphoreType.DMA((chunks,))],
        input_output_aliases={0: 0},
        compiler_params=pltpu.CompilerParams(collective_id=0, has_side_effects=True, vmem_limit_bytes=VMEM_LIMIT),
        cost_estimate=pl.CostEstimate(flops=100_000_000_000, bytes_accessed=100_000_000, transcendentals=0),
        name="multicast",
    )(buf)


def lin_kernel(rows_ref, scale_ref, wq_ref, wk_ref, wv_ref, out_ref):
    normed = rms_norm(rows_ref[...], scale_ref[...])
    n = rows_ref.shape[0]
    at = 0
    for w in (wq_ref, wk_ref, wv_ref):
        y = jnp.dot(normed, w[...], preferred_element_type=jnp.float32).astype(jnp.bfloat16).astype(jnp.float32)
        for j in range(y.shape[1] // 128):
            out_ref[pl.ds(at, n, stride=8), :] = y[:, j * 128:(j + 1) * 128]
            at += 1


def projections(buf, norm_scale, w_query, key_cols, value_cols):
    n, width = buf.shape
    block = 256 if n % 256 == 0 else CHUNK
    full = lambda i: (0, 0)
    return pl.pallas_call(
        lin_kernel,
        grid=(n // block,),
        out_shape=jax.ShapeDtypeStruct((n * 8, 128), jnp.float32),
        in_specs=[
            pl.BlockSpec((block, width), lambda i: (i, 0)),
            pl.BlockSpec((1, width), full),
            pl.BlockSpec(w_query.shape, full),
            pl.BlockSpec(key_cols.shape, full),
            pl.BlockSpec(value_cols.shape, full),
        ],
        out_specs=pl.BlockSpec((block * 8, 128), lambda i: (i, 0)),
        compiler_params=pltpu.CompilerParams(vmem_limit_bytes=VMEM_LIMIT),
        name="projections",
    )(buf, norm_scale.reshape(1, width), w_query, key_cols, value_cols)


TOK = 256


def expand_kernel(slots, lin, cos_ref, sin_ref, q_ref, k_ref, v_ref, store, spread, sem):
    step = pl.program_id(0)

    @pl.when(step == 0)
    def _():
        whole = pltpu.make_async_copy(lin, store, sem)
        whole.start()
        whole.wait()

    def body(b, carry):
        for i in range(32):
            t = b * 32 + i
            at = pl.multiple_of(slots[step * TOK + t], 8)
            spread[pl.ds(pl.multiple_of(t * 8, 8), 8), :] = store[pl.ds(at, 8), :]
        return carry

    lax.fori_loop(0, TOK // 32, body, 0)
    cosines, sines = cos_ref[...], sin_ref[...]
    parts = [spread[pl.ds(j, TOK, stride=8), :] for j in range(6)]
    factor = HEAD_DIM ** -0.5
    half = HEAD_DIM // 2
    q_ref[:, :half] = ((parts[0] * cosines - parts[1] * sines) * factor).astype(q_ref.dtype)
    q_ref[:, half:] = ((parts[1] * cosines + parts[0] * sines) * factor).astype(q_ref.dtype)
    k_ref[:, :half] = (parts[2] * cosines - parts[3] * sines).astype(k_ref.dtype)
    k_ref[:, half:] = (parts[3] * cosines + parts[2] * sines).astype(k_ref.dtype)
    v_ref[:, :half] = parts[4].astype(v_ref.dtype)
    v_ref[:, half:] = parts[5].astype(v_ref.dtype)


def expand(lin, slots, cosines, sines):
    tokens = slots.shape[0]
    head = jax.ShapeDtypeStruct((tokens, HEAD_DIM), jnp.bfloat16)
    out_spec = pl.BlockSpec((TOK, HEAD_DIM), lambda i, s: (i, 0))
    return pl.pallas_call(
        expand_kernel,
        grid_spec=pltpu.PrefetchScalarGridSpec(
            num_scalar_prefetch=1,
            grid=(tokens // TOK,),
            in_specs=[
                pl.BlockSpec(memory_space=pl.ANY),
                pl.BlockSpec((TOK, HEAD_DIM // 2), lambda i, s: (i, 0)),
                pl.BlockSpec((TOK, HEAD_DIM // 2), lambda i, s: (i, 0)),
            ],
            out_specs=[out_spec] * 3,
            scratch_shapes=[pltpu.VMEM(lin.shape, lin.dtype), pltpu.VMEM((TOK * 8, 128), jnp.float32), pltpu.SemaphoreType.DMA],
        ),
        out_shape=(head,) * 3,
        compiler_params=pltpu.CompilerParams(vmem_limit_bytes=VMEM_LIMIT),
        name="expand",
    )(slots * 8, lin, cosines, sines)


def solution(mesh):
    group_size = mesh.shape["tp"]

    def local_step(token_ids, positions, table_rows, norm_scale, w_query, w_key, w_value):
        dev_index = lax.axis_index("tp")
        vocab_rows, model_width = table_rows.shape
        tokens = token_ids.shape[0]
        normalizer = float(np.asarray(math.sqrt(model_width), dtype=jnp.bfloat16))
        kv_heads = w_key.shape[1] // HEAD_DIM
        slot_count = max(kv_heads, group_size)
        slots_here = slot_count // group_size
        first_head = (dev_index * slots_here) // (slot_count // kv_heads)
        if kv_heads * HEAD_DIM == slots_here * HEAD_DIM:
            key_cols, value_cols = w_key, w_value
        else:
            key_cols = lax.dynamic_slice_in_dim(w_key, first_head * HEAD_DIM, slots_here * HEAD_DIM, axis=1)
            value_cols = lax.dynamic_slice_in_dim(w_value, first_head * HEAD_DIM, slots_here * HEAD_DIM, axis=1)

        plan = Plan(group_size, tokens, vocab_rows)
        slots, rows, counts = prepare(plan, group_size, vocab_rows, token_ids)
        slots, rows, counts = slots.reshape(tokens), rows.reshape(-1), counts[:, 0]
        fits = jnp.all(counts <= jnp.asarray(plan.caps, jnp.int32))
        buf = gather_rows(plan, normalizer, counts, rows, table_rows)
        buf = multicast(plan, group_size, buf)

        def fast(buf):
            mine = tokens // group_size
            own = lax.dynamic_slice_in_dim(slots, dev_index * mine, mine)
            residual = own_rows(buf, own)
            lin = projections(buf, norm_scale, w_query, key_cols, value_cols)
            cosines, sines = rope_tables(positions)
            return (residual, *expand(lin, slots, cosines, sines))

        def slow(buf):
            return dense_path(token_ids, positions, table_rows, norm_scale, w_query, key_cols, value_cols)

        residual, queries, key_heads, value_heads = lax.cond(fits, fast, slow, buf)
        return residual, queries[:, None, :], key_heads[:, None, :], value_heads[:, None, :]

    head_spec = P("dp", "tp", None)
    return jax.shard_map(local_step, mesh=mesh, in_specs=(P("dp"), P("dp"), P("tp", None), P(), P(None, "tp"), P(), P()), out_specs=(P(("dp", "tp"), None), head_spec, head_spec, head_spec), check_vma=False)
```

time: 910 us -> 366 us (0.40)
  local copies, waits for them, and re-layouts: 453 us -> 1.45 us
  Pallas kernels: 0 us -> 324 us
  waiting for transfers between devices: 322 us -> 0 us
  matrix products: 51.4 us -> 0 us
  other arithmetic: 58.5 us -> 19.9 us
    gather x1 -> x0, local copies, waits for them, and re-layouts: 439 us -> none  [local_step(): picked = jnp.take(table_rows, local_ids, axis=0, mode='clip') * normalizer]
    pallas_call x0 -> x6, Pallas kernels: none -> 324 us  [the longest x1 172 us: multicast(): pl.pallas_call(functools.partial(multicast_kernel, plan, group_size), out...]
    reduce_scatter x1 -> x0, waiting for transfers between devices: 168 us -> none  [local_step(): residual = lax.psum_scatter(partial, 'tp', scatter_dimension=0, tiled=True)]
    all_gather x1 -> x0, waiting for transfers between devices: 154 us -> none  [local_step(): lax.all_gather(rms_norm(residual, norm_scale), 'tp', axis=0, tiled=True)]
    dot_general x3 -> x0, matrix products: 51.4 us -> none  [the longest x2 35 us: project(): jnp.dot(normed, weight, preferred_element_type=jnp.float32)]
    select_n x1 -> x0, other arithmetic: 22.9 us -> none  [local_step(): partial = jnp.where(inside[:, None], picked, jnp.zeros((), jnp.bfloat16))]
    another operation x1 -> x0, other arithmetic: 20.2 us -> none
    sin x0 -> x1, other arithmetic: none -> 18 us  [rope_tables(): return (jnp.cos(angles), jnp.sin(angles))]
  transfers between devices with their start and end apart: 2 -> 0, of which waited for: 2 -> 0; matrix products, arithmetic and copies ran while one was open for 0% -> 0% of each run, Pallas kernels for 0% -> 0%
where the time goes in v1:
time: 366 us; the launch traced here: 360 us
  Pallas kernels  324 us (89%)
  other arithmetic  19.9 us (5%)
  between operations  14.8 us (4%)
    pallas_call x1, Pallas kernels, multicast(): pl.pallas_call(functools.partial(multicast_kernel, plan, group_size), out...  172 us
    pallas_call x1, Pallas kernels, projections(): pl.pallas_call(lin_kernel, grid=(n // block,), out_shape=jax.ShapeDtypeSt...  87.3 us
    pallas_call x1, Pallas kernels, expand(): pl.pallas_call(expand_kernel, grid_spec=pltpu.PrefetchScalarGridSpec(num_...  35.1 us
    pallas_call x1, Pallas kernels, own_rows(): pl.pallas_call(functools.partial(resid_kernel, count=count), out_shape=ja...  22 us
    sin x1, other arithmetic, rope_tables(): return (jnp.cos(angles), jnp.sin(angles))  18 us

profile of v1, /device:TPU:125, one launch (start us, length us, event | category | flops | bytes accessed | tf_op | source)
XLA Modules:
  0.0 360.1 jit_solution(9933019125599094)
XLA Ops:
  7.2 2.7 slots.1
  9.9 0.8 slice_reduce_fusion.counts
  10.7 0.0 copy-start.8
  10.7 1.3 compare_reduce_fusion
  12.7 0.0 copy-done.8
  12.7 4.3 %owner_rows.1.buf_in = bf16[6016,2048]{1,0:T(8,128)(2,1)} custom-call(s32[8]{0:T(128)} %copy-done.8, s32[3072]{0:T(1024)} %bitcast.29, bf16[32152,2048]{1,0:T(8,128)(2,1)} %table.1), custom_call_target="tpu_custom_call" | custom-call | flops 2952790016 | bytes 100000000 | tf_op jit(solution)/shard_map/owner_rows/pallas_call | solution.py:229
  17.0 0.0 copy-start
  17.0 0.0 copy-start.1
  17.0 0.0 copy-start.2
  17.0 0.0 copy-start.5
  17.0 0.0 copy-start.6
  17.1 0.0 copy-start.7
  17.1 172.3 %multicast.1 = bf16[6016,2048]{1,0:T(8,128)(2,1)} custom-call(bf16[6016,2048]{1,0:T(8,128)(2,1)} %owner_rows.1.buf_in), custom_call_target="tpu_custom_call", output_to_operand_aliasing={{}: (0, {})} | custom-call | flops 99999997952 | bytes 100000000 | tf_op jit(solution)/shard_map/multicast/pallas_call | solution.py:384
  189.4 0.0 copy-done
  189.4 0.0 copy-done.1
  189.4 0.0 copy-done.2
  189.4 0.0 copy-done.5
  189.4 0.0 copy-done.6
  189.4 0.0 copy-done.7
  189.4 163.8 %conditional.1 = (bf16[1024,2048]{1,0:T(8,128)(2,1)}, bf16[8192,1,256]{2,0,1:T(8,128)(2,1)}, bf16[8192,1,256]{2,0,1:T(8,128)(2,1)}, bf16[8192,1,256]{2,0,1:T(8,128)(2,1)}) conditional(s32[]{:T(128)} %convert_element_type.56, (s32[8192]{0:T(1024)S(1)}, bf16[32152,2048]{1,0:T(8,128)(2,1)}, f32[2048]{0:T(1024)S(1)}, bf16[2048,256]{1,0:T(8,128)(2,1)S(1)}, ...), branch_computations={%region_1.4_spmd, %region_4.5_spmd} | conditional | flops 25858994176 | bytes 573859072 | solution.py:520
  189.7 0.6 dynamic_slice.2.rows_smem
  190.3 0.6 broadcast_multiply_fusion.slots
  190.9 22.0 %own_residual.1 = bf16[1024,2048]{1,0:T(8,128)(2,1)} custom-call(s32[1024]{0:T(1024)} %dynamic_slice.2.rows_smem, bf16[6016,2048]{1,0:T(8,128)(2,1)} %get-tuple-element.43.source.rows_ref), custom_call_target="tpu_custom_call" | custom-call | tf_op jit(solution)/shard_map/cond/branch_1_fun/own_residual/pallas_call | solution.py:258
  212.9 87.3 %projections.1.lin = f32[48128,128]{1,0:T(8,128)} custom-call(bf16[6016,2048]{1,0:T(8,128)(2,1)} %get-tuple-element.43.source.rows_ref, f32[1,2048]{1,0:T(1,128)S(1)} %bitcast.28, bf16[2048,256]{1,0:T(8,128)(2,1)S(1)} %get-tuple-element.45.wq_ref, bf16[2048,256]{1,0:T(8,128)(2,1)S(1)} %get-tuple-element.46.wk_ref, bf16[2048,256]{1,0:T(8,128)(2,1)S(1)} %get-tuple-element.47.wv_ref), custom_call_target="tpu_custom_call" | custom-call | tf_op jit(solution)/shard_map/cond/branch_1_fun/projections/pallas_call | solution.py:412
  300.1 18.0 %multiply_sine_fusion = (f32[8192,128]{1,0:T(8,128)}, f32[8192,128]{1,0:T(8,128)}) fusion(f32[128]{0:T(128)S(1)} %multiply_power_fusion, f32[8192]{0:T(1024)S(1)} %convert_element_type.54), kind=kLoop, calls=%fused_computation.1 | loop fusion | flops 1048576 | bytes 8421888 | tf_op jit(solution)/shard_map/cond/branch_1_fun/sin | solution.py:25
  318.1 35.1 %expand.1 = (bf16[8192,256]{1,0:T(8,128)(2,1)}, bf16[8192,256]{1,0:T(8,128)(2,1)}, bf16[8192,256]{1,0:T(8,128)(2,1)}) custom-call(s32[8192]{0:T(1024)} %broadcast_multiply_fusion.slots, f32[48128,128]{1,0:T(8,128)} %projections.1.lin, f32[8192,128]{1,0:T(8,128)} %get-tuple-element.85.cos_ref, f32[8192,128]{1,0:T(8,128)} %get-tuple-element.84.sin_ref), custom_call_target="tpu_custom_call" | custom-call | tf_op jit(solution)/shard_map/cond/branch_1_fun/expand/pallas_call | solution.py:465
  (2 shorter events, 0.0 us)
Async XLA Ops:
  10.7 2.0 copy-start.8
  17.0 172.4 %copy-start = (bf16[2048,256]{1,0:T(8,128)(2,1)S(1)}, bf16[2048,256]{1,0:T(8,128)(2,1)}, u32[]{:S(2)}) copy-start(bf16[2048,256]{1,0:T(8,128)(2,1)} %param.14) | copy-start | bytes 3145732
  17.0 172.4 %copy-start.1 = (bf16[2048,256]{1,0:T(8,128)(2,1)S(1)}, bf16[2048,256]{1,0:T(8,128)(2,1)}, u32[]{:S(2)}) copy-start(bf16[2048,256]{1,0:T(8,128)(2,1)} %param.15) | copy-start | bytes 3145732
  17.0 172.4 %copy-start.2 = (bf16[2048,256]{1,0:T(8,128)(2,1)S(1)}, bf16[2048,256]{1,0:T(8,128)(2,1)}, u32[]{:S(2)}) copy-start(bf16[2048,256]{1,0:T(8,128)(2,1)} %param.16) | copy-start | bytes 3145732
  17.0 172.4 %copy-start.5 = (s32[8192]{0:T(1024)S(1)}, s32[8192]{0:T(1024)}, u32[]{:S(2)}) copy-start(s32[8192]{0:T(1024)} %param.10) | copy-start | bytes 98308
  17.0 172.4 %copy-start.6 = (s32[8192]{0:T(1024)S(1)}, s32[8192]{0:T(1024)}, u32[]{:S(2)}) copy-start(s32[8192]{0:T(1024)} %param.11) | copy-start | bytes 98308
  17.1 172.4 %copy-start.7 = (f32[2048]{0:T(1024)S(1)}, f32[2048]{0:T(1024)}, u32[]{:S(2)}) copy-start(f32[2048]{0:T(1024)} %param.13) | copy-start | bytes 24580
